TPU v7x, 32 devices: a 4x4x1 block of a 4x4x8 slice. The times are simulated.
32 devices in a mesh: batch: 1 (over z), row: 4 (over y), col: 8 (over x, core).
Axes of the slice: x: 4, y: 4, z: 1, core: 2. Of those that a mesh axis runs over, the one named last changes fastest.
The devices are a block of a 4x4x8 slice.
Arguments:
- a_mat: bfloat16 [4096, 65536], P(('batch', 'row'), 'col')
Outputs:
- output: bfloat16 [4096, 4096], P(('batch', 'row'), 'col')
All inputs are finite; a program needn't handle non-finite values.
Results may differ from a plain program's by a relative error of at most 0.001.
Values are sent between devices in bfloat16 or wider.
A program may use at most 768 MiB of HBM per device.

v0:
```python
import jax
import jax.numpy as jnp
from jax import lax
from jax.sharding import PartitionSpec as P

BLOCK = 256


def lower_part(row_panel, col_panel, row_step, row_pos, col_step, col_pos):
    row_blocks = row_panel.shape[0] // BLOCK
    col_blocks = col_panel.shape[0] // BLOCK
    col_total = col_panel.shape[0]
    band_size = max(1, row_blocks // 8)
    col_local = jnp.arange(col_total)
    col_index = ((col_local // BLOCK) * col_step + col_pos) * BLOCK + col_local % BLOCK
    pieces = []
    for first_blk in range(0, row_blocks, band_size):
        last_blk = min(first_blk + band_size, row_blocks)
        col_width = BLOCK * min(col_blocks, (last_blk * row_step - 1) // col_step + 1)
        product = lax.dot_general(row_panel[first_blk * BLOCK:last_blk * BLOCK], col_panel[:col_width], (((1,), (1,)), ((), ())), preferred_element_type=jnp.float32)
        row_local = jnp.arange(first_blk * BLOCK, last_blk * BLOCK)
        row_index = ((row_local // BLOCK) * row_step + row_pos) * BLOCK + row_local % BLOCK
        kept_vals = jnp.where(row_index[:, None] >= col_index[None, :col_width], product, 0.0).astype(jnp.bfloat16)
        pieces.append(jnp.pad(kept_vals, ((0, 0), (0, col_total - col_width))))
    return jnp.concatenate(pieces, axis=0)


def solution(mesh):
    row_count = mesh.shape['row']
    col_count = mesh.shape['col']

    def local_fn(a_local):
        local_rows, m_local = a_local.shape
        n_total = local_rows * row_count
        row_pos = lax.axis_index('row')
        col_pos = lax.axis_index('col')
        row_panel = lax.all_gather(a_local, 'col', axis=1, tiled=True)
        gathered = lax.all_gather(a_local.reshape(local_rows // BLOCK, BLOCK, m_local), 'row', axis=1)
        grouped = gathered.reshape(n_total // (BLOCK * col_count), col_count, BLOCK, m_local)
        swapped = lax.all_to_all(grouped, 'col', 1, 3, tiled=True)
        col_panel = swapped.reshape(n_total // col_count, m_local * col_count)
        return lower_part(row_panel, col_panel, row_count, row_pos, col_count, col_pos)

    part_spec = P(('batch', 'row'), 'col')
    return jax.shard_map(local_fn, mesh=mesh, in_specs=(part_spec,), out_specs=part_spec, check_vma=False)
```

profile of v0, /device:TPU:98, one launch (start us, length us, event | category | flops | bytes accessed | tf_op | source)
XLA Modules:
  0.0 2243.4 jit_solution(18158250019067571193)
XLA Ops:
  6.5 0.0 all-gather.5.cloned.1.call-start
  6.6 0.7 all-gather.5.cloned.1.call-update
  7.3 0.1 all-gather.3.cloned.1.call-start
  7.4 0.7 all-gather.3.cloned.1.call-update
  8.1 574.3 %all-gather.5.cloned.1.call-done = bf16[4,4,256,8192]{3,2,1,0:T(8,128)(2,1)} async-done(((bf16[4,1,256,8192]{3,2,1,0:T(8,128)(2,1)}), bf16[4,4,256,8192]{3,2,1,0:T(8,128)(2,1)}) %all-gather.5.cloned.1.call-update) | async-done | bytes 67108880 | tf_op jit(solution)/shard_map/all_gather | solution.py:38
  582.4 44.6 %copy.4 = bf16[2,8,256,8192]{3,2,0,1:T(8,128)(2,1)} copy(bf16[2,8,256,8192]{3,2,1,0:T(8,128)(2,1)} %bitcast.1) | data formatting | bytes 134217728 | tf_op jit(solution)/shard_map/reshape | solution.py:39
  627.0 10.3 all-to-all-start
  637.3 0.0 copy-start
  637.3 0.6 copy-done
  637.9 0.6 fusion.51
  638.4 0.6 fusion.53
  639.0 1235.9 %all-to-all-done = bf16[2,8,256,8192]{3,2,0,1:T(8,128)(2,1)} async-done(((bf16[2,8,256,8192]{3,2,0,1:T(8,128)(2,1)}), bf16[2,8,256,8192]{3,2,0,1:T(8,128)(2,1)}, u32[]{:S(2)}, u32[]{:S(2)}) %all-to-all-start) | async-done | bytes 67108896 | tf_op jit(solution)/shard_map/all_to_all | solution.py:40
  1875.0 82.5 %copy.5 = bf16[2,8,256,8192]{2,3,1,0:T(8,128)(2,1)} copy(bf16[2,8,256,8192]{3,2,0,1:T(8,128)(2,1)} %all-to-all-done) | data formatting | bytes 134217728 | tf_op jit(solution)/shard_map/all_to_all | solution.py:40
  1957.5 22.8 %slice.31 = bf16[1,1,256,8,8192]{2,4,3,1,0:T(8,128)(2,1)} slice(bf16[2,1,256,8,8192]{2,4,3,1,0:T(8,128)(2,1)} %bitcast.3), slice={[0:1], [0:1], [0:256], [0:8], [0:8192]} | slice | bytes 67108864 | tf_op jit(solution)/shard_map/slice | solution.py:20
  1980.3 85.5 %copy.6 = bf16[2,1,256,8,8192]{4,3,2,0,1:T(8,128)(2,1)} copy(bf16[2,1,256,8,8192]{2,4,3,1,0:T(8,128)(2,1)} %bitcast.3) | data formatting | bytes 134217728 | tf_op jit(solution)/shard_map/all_to_all | solution.py:40
  2065.8 55.5 %copy.7 = bf16[64,8,8,8192]{3,1,2,0:T(8,128)(2,1)} copy(bf16[64,8,8,8192]{3,2,1,0:T(8,128)(2,1)} %bitcast.8) | data formatting | bytes 134217728
  2121.3 0.0 all-gather.3.cloned.1.call-done
  2121.3 0.0 copy-start.4
  2121.3 23.6 %fusion.32 = bf16[256,256]{1,0:T(8,128)(2,1)S(1)} fusion(bf16[256,65536]{0,1:T(8,128)(2,1)} %bitcast.15, bf16[1024,65536]{1,0:T(8,128)(2,1)} %all-gather.3.cloned.1.call-done, s32[256]{0:T(256)S(1)} %slice.23, s32[256]{0:T(256)S(1)} %get-tuple-element.6), kind=kOutput, calls=%fused_computation.21 | convolution fusion | flops 8590131200 | bytes 67241984 | tf_op jit(solution)/shard_map/dot_general | solution.py:20
  2144.9 0.0 copy-done.4
  2144.9 0.0 copy-start.1
  2144.9 0.0 copy-start.3
  2144.9 23.6 %fusion.26 = bf16[256,256]{1,0:T(8,128)(2,1)S(1)} fusion(bf16[256,65536]{0,1:T(8,128)(2,1)} %bitcast.16, bf16[1024,65536]{1,0:T(8,128)(2,1)} %all-gather.3.cloned.1.call-done, s32[256]{0:T(256)S(1)} %slice.23, s32[256]{0:T(256)S(1)} %copy-done.4), kind=kOutput, calls=%fused_computation.19 | convolution fusion | flops 8590131200 | bytes 67241984 | tf_op jit(solution)/shard_map/dot_general | solution.py:20
  2168.5 0.0 copy-done.1
  2168.5 0.0 copy-done.3
  2168.5 0.0 copy-start.2
  2168.5 33.5 %fusion.17 = bf16[256,512]{1,0:T(8,128)(2,1)S(1)} fusion(bf16[512,65536]{1,0:T(8,128)(2,1)} %bitcast.9, bf16[1024,65536]{1,0:T(8,128)(2,1)} %all-gather.3.cloned.1.call-done, s32[512]{0:T(512)S(1)} %copy-done.1, s32[256]{0:T(256)S(1)} %copy-done.3), kind=kOutput, calls=%fused_computation.16 | convolution fusion | flops 17180262400 | bytes 100928512 | tf_op jit(solution)/shard_map/dot_general | solution.py:20
  2202.0 0.0 copy-done.2
  2202.0 33.5 %fusion.20 = bf16[256,512]{1,0:T(8,128)(2,1)S(1)} fusion(bf16[512,65536]{1,0:T(8,128)(2,1)} %bitcast.9, bf16[1024,65536]{1,0:T(8,128)(2,1)} %all-gather.3.cloned.1.call-done, s32[512]{0:T(512)S(1)} %copy-done.1, s32[256]{0:T(256)S(1)} %copy-done.2), kind=kOutput, calls=%fused_computation.17 | convolution fusion | flops 17180262400 | bytes 100928512 | tf_op jit(solution)/shard_map/dot_general | solution.py:20
  2235.5 1.0 fusion.37
  (2 shorter events, 0.0 us)
Async XLA Ops:
  6.5 575.8 %all-gather.5.cloned.1.call-start = ((), (), s32[]{:S(2)}) async-start(), calls=%async_computation.2 | async-start | bytes 83886080 | tf_op jit(solution)/shard_map/all_gather | solution.py:38
  7.3 2114.0 %all-gather.3.cloned.1.call-start = ((), (), s32[]{:S(2)}) async-start(), calls=%async_computation.1 | async-start | bytes 150994944 | tf_op jit(solution)/shard_map/all_gather | solution.py:37
  627.0 1248.0 %all-to-all-start = ((bf16[2,8,256,8192]{3,2,0,1:T(8,128)(2,1)}), bf16[2,8,256,8192]{3,2,0,1:T(8,128)(2,1)}, u32[]{:S(2)}, u32[]{:S(2)}) async-start(bf16[2,8,256,8192]{3,2,0,1:T(8,128)(2,1)} %copy.4), calls=%async_computation | async-start | bytes 134217728 | tf_op jit(solution)/shard_map/all_to_all | solution.py:40
  637.3 0.6 copy-start
  2121.3 23.6 %copy-start.4 = (s32[256]{0:T(256)S(1)}, s32[256]{0:T(256)}, u32[]{:S(2)}) copy-start(s32[256]{0:T(256)} %get-tuple-element.5) | copy-start | bytes 3076
  2144.9 23.6 %copy-start.1 = (s32[512]{0:T(512)S(1)}, s32[512]{0:T(512)}, u32[]{:S(2)}) copy-start(s32[512]{0:T(512)} %copy-done) | copy-start | bytes 6148
  2144.9 23.6 %copy-start.3 = (s32[256]{0:T(256)S(1)}, s32[256]{0:T(256)}, u32[]{:S(2)}) copy-start(s32[256]{0:T(256)} %get-tuple-element.8) | copy-start | bytes 3076
  2168.5 33.5 %copy-start.2 = (s32[256]{0:T(256)S(1)}, s32[256]{0:T(256)}, u32[]{:S(2)}) copy-start(s32[256]{0:T(256)} %get-tuple-element.7) | copy-start | bytes 3076
Sparse Core Ops, SparseCore 0:
  8.9 573.4 all-gather.4
  584.0 1259.6 all-gather.2
where the time goes:
time: 2250 us; the launch traced here: 2240 us
  waiting for transfers between devices  1810 us (80%)
  local copies, waits for them, and re-layouts  291 us (13%)
  matrix products  114 us (5%)
    all_to_all x1, waiting for transfers between devices, local_fn(): swapped = lax.all_to_all(grouped, 'col', 1, 3, tiled=True)  1240 us
    all_gather x1, waiting for transfers between devices, local_fn(): lax.all_gather(a_local.reshape(local_rows // BLOCK, BLOCK, m_local), 'row...  574 us
    all_to_all x2, local copies, waits for them, and re-layouts, local_fn(): swapped = lax.all_to_all(grouped, 'col', 1, 3, tiled=True)  168 us
    dot_general x4, matrix products, lower_part(): lax.dot_general(row_panel[first_blk * BLOCK:last_blk * BLOCK], col_panel[...  114 us
    unnamed x11, local copies, waits for them, and re-layouts  56.1 us
  transfers between devices with their start and end apart: 3, of which 2 were waited for; matrix products, arithmetic and copies ran while one was open for 13% of the time, Pallas kernels for 0%

commit v1 on v0

v1 whole, which is shorter than its diff:
```python
import functools

import jax
import jax.numpy as jnp
from jax import lax
from jax.experimental import pallas as pl
from jax.experimental.pallas import tpu as pltpu
from jax.sharding import PartitionSpec as P

BLOCK = 256
HALF = BLOCK // 2
QUART = BLOCK // 4
MESH = pl.DeviceIdType.MESH
F32 = jnp.float32


def kernel(rows, cols, a_ref, c_ref, relay, xin, part, xmid, xdst, red, ymid, ydst,
           d_s, d_r, r_s, r_r, f_s, f_r, loc_s, core_s, core_r,
           xm_s, xm_r, xo_s, xo_r, xa_s, xa_r, ym_s, ym_r, yo_s, yo_r, ya_s, ya_r, credit):
    chips = cols // 2
    y = lax.axis_index("row")
    pos = lax.axis_index("col")
    x, core = lax.div(pos, 2), lax.rem(pos, 2)
    local_rows, m_local = a_ref.shape
    width = m_local // rows
    half_w = width // 2
    steps = local_rows // HALF
    ents = xdst.shape[2]

    def yy(o):
        return lax.rem(y + o, rows)

    def xx(o):
        return lax.rem(x + o, chips)

    up, down = {"row": yy(1)}, {"row": yy(rows - 1)}
    right, left = {"col": 2 * xx(1) + core}, {"col": 2 * xx(chips - 1) + core}
    twin = {"col": 2 * x + 1 - core}
    ydev, xdev = (up, down), (right, left)

    def remote(src, dst, s, r, dev):
        return pltpu.make_async_remote_copy(
            src_ref=src, dst_ref=dst, send_sem=s, recv_sem=r, device_id=dev, device_id_type=MESH)

    def arrived(dst, s, r):
        remote(dst, dst, s, r, twin).wait_recv()

    def left_us(src, s, r):
        remote(src, src, s, r, twin).wait_send()

    barrier = pltpu.get_barrier_semaphore()
    for dev in (up, down, right, left, twin):
        pl.semaphore_signal(barrier, inc=1, device_id=dev, device_id_type=MESH)
    pl.semaphore_wait(barrier, 5)

    def a_piece(h, owner, off, size):
        return a_ref.at[pl.ds(pl.multiple_of(h * HALF, HALF), HALF),
                        pl.ds(pl.multiple_of(owner * width + off, 128), size)]

    def x_piece(h, group, off, size):
        return xin.at[lax.div(h, 2), group, pl.ds(pl.multiple_of(lax.rem(h, 2) * HALF, HALF), HALF), pl.ds(off, size)]

    def direct(h, d):
        return remote(a_piece(h, yy(1 if d == 0 else rows - 1), 0, width), x_piece(h, y, 0, width),
                      d_s.at[d, h], d_r.at[d, h], ydev[d])

    def relay_out(h, d):
        return remote(a_piece(h, yy(2), d * half_w, half_w), relay.at[d, h], r_s.at[d, h], r_r.at[d, h], ydev[d])

    def forward(h, d):
        return remote(relay.at[d, h], x_piece(h, yy(rows - 1 if d == 0 else 1), d * half_w, half_w),
                      f_s.at[d, h], f_r.at[d, h], ydev[d])

    def own(h):
        return pltpu.make_async_copy(a_piece(h, y, 0, width), x_piece(h, y, 0, width), loc_s.at[h])

    def twin_rows(h, off):
        half = pl.ds(pl.multiple_of(lax.rem(h, 2) * HALF, HALF), HALF)
        return xin.at[lax.div(h, 2), :, half, pl.ds(off, width)]

    def to_twin(h):
        return remote(twin_rows(h, 0), twin_rows(h, width), core_s.at[h], core_r.at[h], twin)

    def both(f, h):
        for d in range(2):
            f(h, d).start()

    def pass_on(h):
        for d in range(2):
            arrived(relay.at[d, h], r_s.at[d, h], r_r.at[d, h])
        both(forward, h)

    def have(h):
        own(h).wait()
        for d in range(2):
            arrived(x_piece(h, yy(rows - 1 if d == 0 else 1), 0, width), d_s.at[d, h], d_r.at[d, h])
            arrived(x_piece(h, yy(2), d * half_w, half_w), f_s.at[d, h], f_r.at[d, h])

    def split(t):
        w, kind = lax.div(t, 3), lax.rem(t, 3)
        return w, kind, lax.div(kind, 2)

    def place(t, e):
        w, kind, own_cols = split(t)
        return 2 * w + (1 - own_cols) * kind + own_cols * e, (1 - own_cols) * e + own_cols * lax.div(2 * w, chips)

    def column(t, o, e):
        return chips * place(t, e)[1] + xx(o)

    def low(t, o, e):
        w, _, own_cols = split(t)
        m = column(t, o, e)
        return ((own_cols == 0) & (m < 2 * w)) | ((own_cols == 1) & (m == 2 * w))

    def high(t, o, e):
        w, _, own_cols = split(t)
        m = column(t, o, e)
        return ((own_cols == 0) & (m < 2 * w)) | ((own_cols == 1) & (lax.div(m, 2) == w))

    A, B = pl.ds(0, 2), pl.ds(2, 2)

    def x_mid(t, e, d):
        sl = lax.rem(t, 2)
        return remote(part.at[sl, 1, e, (A, B)[d]], xmid.at[sl, d, e],
                      xm_s.at[d, sl, e], xm_r.at[d, sl, e], xdev[d])

    def x_own(t, e, d):
        sl, half = lax.rem(t, 2), (B, A)[d]
        return remote(part.at[sl, 2 * d, e, half], xdst.at[sl, d, e, half],
                      xo_s.at[d, sl, e], xo_r.at[d, sl, e], xdev[d])

    def x_acc(t, e, d):
        sl, half = lax.rem(t, 2), (A, B)[d]
        return remote(part.at[sl, 2 * d, e, half], xdst.at[sl, d, e, half],
                      xa_s.at[d, sl, e], xa_r.at[d, sl, e], xdev[d])

    def compute(t, o):
        w, sl = lax.div(t, 3), lax.rem(t, 2)

        def one(e, _):
            @pl.when(high(t, o, e))
            def _():
                h, cb = place(t, e)
                j = 2 * column(t, o, e) + core
                sub = pl.ds(pl.multiple_of(lax.rem(h, 2) * HALF, HALF), HALF)
                lhs = xin[w, :, sub, :].reshape(rows * HALF, 2 * width)
                rhs = xin[lax.div(j, rows), lax.rem(j, rows)]
                val = lax.dot_general(lhs, rhs, (((1,), (1,)), ((), ())), preferred_element_type=F32)
                val = val.reshape(rows, HALF, BLOCK)
                if o == 0:
                    red[h, cb] = val
                else:
                    part[sl, o - 1, e] = val
            return 0

        lax.fori_loop(0, ents, one, 0)

    def x_send_mid(t):
        for e in range(ents):
            @pl.when(low(t, 2, e))
            def _():
                x_mid(t, e, 0).start()

            @pl.when(high(t, 2, e))
            def _():
                x_mid(t, e, 1).start()

    def x_send_own(t, d):
        for e in range(ents):
            @pl.when(high(t, 1, e) if d == 0 else low(t, chips - 1, e))
            def _():
                x_own(t, e, d).start()

    def x_pass_on(t):
        sl = lax.rem(t, 2)
        for e in range(ents):
            @pl.when(low(t, 1, e))
            def _():
                arrived(xmid.at[sl, 0, e], xm_s.at[0, sl, e], xm_r.at[0, sl, e])
                part[sl, 0, e, A] += xmid[sl, 0, e]
                x_acc(t, e, 0).start()

            @pl.when(high(t, chips - 1, e))
            def _():
                arrived(xmid.at[sl, 1, e], xm_s.at[1, sl, e], xm_r.at[1, sl, e])
                part[sl, 2, e, B] += xmid[sl, 1, e]
                x_acc(t, e, 1).start()

    def x_finish(t):
        sl = lax.rem(t, 2)
        for e in range(ents):
            h, cb = place(t, e)

            @pl.when(low(t, 0, e))
            def _():
                arrived(xdst.at[sl, 0, e, A], xa_s.at[0, sl, e], xa_r.at[0, sl, e])
                arrived(xdst.at[sl, 1, e, A], xo_s.at[1, sl, e], xo_r.at[1, sl, e])
                red[h, cb, A] = red[h, cb, A] + xdst[sl, 0, e, A] + xdst[sl, 1, e, A]

            @pl.when(high(t, 0, e))
            def _():
                arrived(xdst.at[sl, 0, e, B], xo_s.at[0, sl, e], xo_r.at[0, sl, e])
                arrived(xdst.at[sl, 1, e, B], xa_s.at[1, sl, e], xa_r.at[1, sl, e])
                red[h, cb, B] = red[h, cb, B] + xdst[sl, 0, e, B] + xdst[sl, 1, e, B]

    def x_sent(t):
        sl = lax.rem(t, 2)
        for e in range(ents):
            for o, d, half, s, r, test in (
                    (2, 0, A, xm_s, xm_r, low), (2, 1, B, xm_s, xm_r, high),
                    (1, 0, B, xo_s, xo_r, high), (chips - 1, 1, A, xo_s, xo_r, low),
                    (1, 0, A, xa_s, xa_r, low), (chips - 1, 1, B, xa_s, xa_r, high)):
                @pl.when(test(t, o, e))
                def _():
                    left_us(part.at[sl, o - 1, e, half], s.at[d, sl, e], r.at[d, sl, e])

    def give_credit():
        pl.semaphore_signal(credit.at[0], inc=1, device_id=left, device_id_type=MESH)
        pl.semaphore_signal(credit.at[1], inc=1, device_id=right, device_id_type=MESH)

    def take_credit():
        pl.semaphore_wait(credit.at[0], 1)
        pl.semaphore_wait(credit.at[1], 1)

    T, U = pl.ds(0, QUART), pl.ds(QUART, QUART)

    def exists(t, o, e):
        w, _, own_cols = split(t)
        m = column(t, 0, e)
        return ((own_cols == 0) & (m < 2 * w)) | (
            (own_cols == 1) & (lax.div(m, 2) == w) & (rows * w + yy(o) >= 2 * m + core))

    def y_mid(h, cb, d):
        return remote(red.at[h, cb, yy(2), (T, U)[d]], ymid.at[h, d, cb],
                      ym_s.at[d, h, cb], ym_r.at[d, h, cb], ydev[d])

    def y_own(h, cb, d):
        half = (U, T)[d]
        return remote(red.at[h, cb, yy((1, rows - 1)[d]), half], ydst.at[h, d, cb, half],
                      yo_s.at[d, h, cb], yo_r.at[d, h, cb], ydev[d])

    def y_acc(h, cb, d):
        half = (T, U)[d]
        return remote(red.at[h, cb, yy((1, rows - 1)[d]), half], ydst.at[h, d, cb, half],
                      ya_s.at[d, h, cb], ya_r.at[d, h, cb], ydev[d])

    def y_send(t):
        for e in range(ents):
            h, cb = place(t, e)

            @pl.when(exists(t, 2, e))
            def _():
                for d in range(2):
                    y_mid(h, cb, d).start()
        for e in range(ents):
            h, cb = place(t, e)
            for d in range(2):
                @pl.when(exists(t, (1, rows - 1)[d], e))
                def _():
                    y_own(h, cb, d).start()

    def y_pass_on(t):
        for e in range(ents):
            h, cb = place(t, e)
            for d in range(2):
                o, half = (1, rows - 1)[d], (T, U)[d]

                @pl.when(exists(t, o, e))
                def _():
                    arrived(ymid.at[h, d, cb], ym_s.at[d, h, cb], ym_r.at[d, h, cb])
                    red[h, cb, yy(o), half] += ymid[h, d, cb]
                    y_acc(h, cb, d).start()

    def y_finish(t):
        for e in range(ents):
            h, cb = place(t, e)

            @pl.when(exists(t, 0, e))
            def _():
                for d in range(2):
                    half, other = (U, T)[d], (T, U)[d]
                    arrived(ydst.at[h, d, cb, half], yo_s.at[d, h, cb], yo_r.at[d, h, cb])
                    arrived(ydst.at[h, d, cb, other], ya_s.at[d, h, cb], ya_r.at[d, h, cb])
                val = red[h, cb, y] + ydst[h, 0, cb] + ydst[h, 1, cb]
                shape = (HALF, BLOCK)
                i = (rows * lax.div(h, 2) + y) * BLOCK + lax.rem(h, 2) * HALF + lax.broadcasted_iota(jnp.int32, shape, 0)
                j = (cols * cb + pos) * BLOCK + lax.broadcasted_iota(jnp.int32, shape, 1)
                c_ref[pl.ds(pl.multiple_of(h * HALF, HALF), HALF), pl.ds(pl.multiple_of(cb * BLOCK, BLOCK), BLOCK)] = (
                    jnp.where(i >= j, val, 0.0).astype(c_ref.dtype))

    def y_sent(t):
        for e in range(ents):
            h, cb = place(t, e)
            for d in range(2):
                o, half, other = (1, rows - 1)[d], (U, T)[d], (T, U)[d]

                @pl.when(exists(t, 2, e))
                def _():
                    left_us(red.at[h, cb, yy(2), other], ym_s.at[d, h, cb], ym_r.at[d, h, cb])

                @pl.when(exists(t, o, e))
                def _():
                    left_us(red.at[h, cb, yy(o), half], yo_s.at[d, h, cb], yo_r.at[d, h, cb])
                    left_us(red.at[h, cb, yy(o), other], ya_s.at[d, h, cb], ya_r.at[d, h, cb])

    def loop(lo, hi, f):
        def body(i, _):
            f(i)
            return 0
        lax.fori_loop(lo, hi, body, 0)

    both(relay_out, 0)
    both(relay_out, 1)
    both(direct, 0)
    loop(0, steps, lambda h: own(h).start())
    c_ref[...] = jnp.zeros_like(c_ref)
    pass_on(0)
    both(relay_out, 2)
    both(direct, 1)
    pass_on(1)
    both(relay_out, 3)
    items = 3 * steps // 2

    def step(t):
        w, kind = lax.div(t, 3), lax.rem(t, 3)
        h = 2 * w + kind

        @pl.when(kind < 2)
        def _():
            have(h)
            to_twin(h).start()

            @pl.when(h + 2 < steps)
            def _():
                pass_on(h + 2)
                both(direct, h + 2)

            @pl.when(h + 4 < steps)
            def _():
                both(relay_out, h + 4)

        @pl.when(t >= 2)
        def _():
            x_finish(t - 2)
            give_credit()

        @pl.when(t >= 1)
        def _():
            x_pass_on(t - 1)

        @pl.when(t >= 2)
        def _():
            x_sent(t - 2)

        @pl.when(kind < 2)
        def _():
            arrived(twin_rows(h, width), core_s.at[h], core_r.at[h])
        compute(t, 2)

        @pl.when(t >= 2)
        def _():
            take_credit()
        x_send_mid(t)
        compute(t, 1)
        x_send_own(t, 0)
        compute(t, chips - 1)
        x_send_own(t, 1)
        compute(t, 0)

    loop(0, items, step)

    early = items - 2
    loop(0, early, y_send)
    x_finish(items - 2)
    x_pass_on(items - 1)
    y_send(items - 2)
    loop(0, early, y_pass_on)
    y_pass_on(items - 2)
    x_finish(items - 1)
    y_send(items - 1)
    loop(0, early, y_finish)
    y_finish(items - 2)
    y_pass_on(items - 1)
    y_finish(items - 1)

    def drain(h):
        for d in range(2):
            left_us(a_piece(h, yy(1), 0, width), d_s.at[d, h], d_r.at[d, h])
            left_us(a_piece(h, yy(2), 0, half_w), r_s.at[d, h], r_r.at[d, h])
            left_us(relay.at[d, h], f_s.at[d, h], f_r.at[d, h])
        left_us(twin_rows(h, 0), core_s.at[h], core_r.at[h])

    x_sent(items - 2)
    x_sent(items - 1)
    loop(0, steps, drain)
    loop(0, items, y_sent)


def solution(mesh):
    rows, cols = mesh.shape["row"], mesh.shape["col"]

    def local_fn(a_local):
        local_rows, m_local = a_local.shape
        steps, waves = local_rows // HALF, local_rows // BLOCK
        width = m_local // rows
        chips = cols // 2
        cbs = local_rows * rows // (BLOCK * cols)
        dma = pltpu.SemaphoreType.DMA
        c, _ = pl.pallas_call(
            functools.partial(kernel, rows, cols),
            out_shape=(
                jax.ShapeDtypeStruct((local_rows, cbs * BLOCK), a_local.dtype),
                jax.ShapeDtypeStruct((2, steps, HALF, width // 2), a_local.dtype),
            ),
            in_specs=[pl.BlockSpec(memory_space=pltpu.HBM)],
            out_specs=(pl.BlockSpec(memory_space=pltpu.VMEM), pl.BlockSpec(memory_space=pltpu.HBM)),
            scratch_shapes=[
                pltpu.VMEM((waves, rows, BLOCK, 2 * width), a_local.dtype),
                pltpu.VMEM((2, chips - 1, cbs, rows, HALF, BLOCK), F32),
                pltpu.VMEM((2, 2, cbs, 2, HALF, BLOCK), F32),
                pltpu.VMEM((2, 2, cbs, rows, HALF, BLOCK), F32),
                pltpu.VMEM((steps, cbs, rows, HALF, BLOCK), F32),
                pltpu.VMEM((steps, 2, cbs, QUART, BLOCK), F32),
                pltpu.VMEM((steps, 2, cbs, HALF, BLOCK), F32),
            ] + [dma((2, steps))] * 6 + [dma((steps,))] * 3 + [dma((2, 2, cbs))] * 6
            + [dma((2, steps, cbs))] * 6 + [pltpu.SemaphoreType.REGULAR((2,))],
            compiler_params=pltpu.CompilerParams(
                collective_id=0, has_side_effects=True, vmem_limit_bytes=67043328),
        )(a_local)
        return c

    spec = P(("batch", "row"), "col")
    return jax.shard_map(local_fn, mesh=mesh, in_specs=(spec,), out_specs=spec, check_vma=False)
```

time: 2250 us -> 307 us (0.14)
  the two profiles are of different devices: /device:TPU:98 before, /device:TPU:104 now
where the time goes in v1:
time: 307 us
  Pallas kernels  305 us (99%)
    pallas_call x1, Pallas kernels, local_fn(): pl.pallas_call(functools.partial(kernel, rows, cols), out_shape=(jax.Shap...  305 us

profile of v1, /device:TPU:104, one launch (start us, length us, event | category | flops | bytes accessed | tf_op | source)
XLA Modules:
  0.0 307.2 jit_solution(4626663731605931014)
XLA Ops:
  0.0 304.9 %shard_map.17 = (bf16[1024,512]{1,0:T(8,128)(2,1)}, bf16[2,8,128,1024]{3,2,1,0:T(8,128)(2,1)}) custom-call(bf16[1024,8192]{1,0:T(8,128)(2,1)} %a_ref.1), custom_call_target="tpu_custom_call" | custom-call | tf_op jit(solution)/shard_map/pallas_call | solution.py:409
  305.0 2.3 copy.3

commit v2 on v0

v2 whole, which is shorter than its diff:
```python
import functools

import jax
import jax.numpy as jnp
from jax import lax
from jax.experimental import pallas as pl
from jax.experimental.pallas import tpu as pltpu
from jax.sharding import PartitionSpec as P

BLOCK = 256
HALF = BLOCK // 2
QUART = BLOCK // 4
MESH = pl.DeviceIdType.MESH
F32 = jnp.float32
START = 8
TAIL = (
    "S5", "H9", "p7", "C8", "S2", "G9", "f6", "C9", "S3", "H10", "f7", "S7", "S4", "P3", "p8", "S6", "p9",
    "C10", "P5", "f8", "Z0", "F5", "P4", "P2", "p10", "f9", "F3", "S8", "Z1", "P6", "F2", "P8", "S9", "f10",
    "S10", "Z2", "P9", "Z3", "F4", "P10", "P7", "F9", "F8", "F6", "F10", "Z4", "F7",
)


def kernel(rows, cols, a_ref, c_ref, relay, xin, part, xmid, xdst, red, ymid, ydst, fin,
           d_s, d_r, r_s, r_r, f_s, f_r, loc_s, core_s, core_r,
           xm_s, xm_r, xo_s, xo_r, xa_s, xa_r, ym_s, ym_r, yo_s, yo_r, ya_s, ya_r,
           zm_s, zm_r, zo_s, zo_r, za_s, za_r, wm_s, wm_r, wo_s, wo_r, wa_s, wa_r, fin_s, fin_r, credit):
    chips = cols // 2
    y = lax.axis_index("row")
    pos = lax.axis_index("col")
    x, core = lax.div(pos, 2), lax.rem(pos, 2)
    local_rows, m_local = a_ref.shape
    width = m_local // rows
    half_w = width // 2
    steps = local_rows // HALF
    items = 3 * steps // 2
    last = steps // 2 - 1
    late = steps - steps // 2
    slots, ents = part.shape[0], part.shape[2]

    def div(p, q):
        return p // q if isinstance(p, int) else lax.div(p, q)

    def rem(p, q):
        return p % q if isinstance(p, int) else lax.rem(p, q)

    def when(test, f):
        if isinstance(test, bool):
            if test:
                f()
        else:
            pl.when(test)(f)

    def yy(o):
        return lax.rem(y + o, rows)

    def xx(o):
        return lax.rem(x + o, chips)

    up, down = {"row": yy(1)}, {"row": yy(rows - 1)}
    right, left = {"col": 2 * xx(1) + core}, {"col": 2 * xx(chips - 1) + core}
    across = {"col": 2 * xx(2) + core}
    twin = {"col": 2 * x + 1 - core}
    ydev, xdev = (up, down), (right, left)

    def remote(src, dst, s, r, dev):
        return pltpu.make_async_remote_copy(
            src_ref=src, dst_ref=dst, send_sem=s, recv_sem=r, device_id=dev, device_id_type=MESH)

    def arrived(dst, s, r):
        remote(dst, dst, s, r, twin).wait_recv()

    def left_us(src, s, r):
        remote(src, src, s, r, twin).wait_send()

    def signal(sem, dev):
        pl.semaphore_signal(sem, inc=1, device_id=dev, device_id_type=MESH)

    barrier = pltpu.get_barrier_semaphore()
    for dev in (up, down, right, left, across, twin):
        signal(barrier, dev)
    pl.semaphore_wait(barrier, 6)

    def half_rows(h):
        return pl.ds(pl.multiple_of(rem(h, 2) * HALF, HALF), HALF)

    def a_piece(h, owner, off, size):
        return a_ref.at[pl.ds(pl.multiple_of(h * HALF, HALF), HALF),
                        pl.ds(pl.multiple_of(owner * width + off, 128), size)]

    def x_piece(h, group, off, size):
        return xin.at[div(h, 2), group, half_rows(h), pl.ds(off, size)]

    def direct(h, d):
        return remote(a_piece(h, yy(1 if d == 0 else rows - 1), 0, width), x_piece(h, y, 0, width),
                      d_s.at[d, h], d_r.at[d, h], ydev[d])

    def relay_out(h, d):
        return remote(a_piece(h, yy(2), d * half_w, half_w), relay.at[d, h], r_s.at[d, h], r_r.at[d, h], ydev[d])

    def forward(h, d):
        return remote(relay.at[d, h], x_piece(h, yy(rows - 1 if d == 0 else 1), d * half_w, half_w),
                      f_s.at[d, h], f_r.at[d, h], ydev[d])

    def own(h):
        return pltpu.make_async_copy(a_piece(h, y, 0, width), x_piece(h, y, 0, width), loc_s.at[h])

    def twin_rows(h, off):
        return xin.at[div(h, 2), :, half_rows(h), pl.ds(off, width)]

    def to_twin(h):
        return remote(twin_rows(h, 0), twin_rows(h, width), core_s.at[h], core_r.at[h], twin)

    def both(f, h):
        for d in range(2):
            f(h, d).start()

    def pass_on(h):
        for d in range(2):
            arrived(relay.at[d, h], r_s.at[d, h], r_r.at[d, h])
        both(forward, h)

    def split(t):
        w, kind = div(t, 3), rem(t, 3)
        return w, kind, div(kind, 2)

    def choose(own_cols, before, inside):
        if isinstance(own_cols, int):
            return inside if own_cols else before
        return ((own_cols == 0) & before) | ((own_cols == 1) & inside)

    def place(t, e):
        w, kind, own_cols = split(t)
        return 2 * w + (1 - own_cols) * kind + own_cols * e, (1 - own_cols) * e + own_cols * div(2 * w, chips)

    def spot(t, e):
        h, cb = place(t, e)
        return h + late * cb

    def moved(t):
        return isinstance(t, int) and t // 3 == last and t % 3 < 2

    def column(t, o, e):
        return chips * place(t, e)[1] + xx(o + 2 * e if moved(t) else o)

    def low(t, o, e):
        w, _, own_cols = split(t)
        m = column(t, o, e)
        return choose(own_cols, m < 2 * w, m == 2 * w)

    def high(t, o, e):
        w, _, own_cols = split(t)
        m = column(t, o, e)
        return choose(own_cols, m < 2 * w, lax.div(m, 2) == w)

    A, B = pl.ds(0, 2), pl.ds(2, 2)

    def product(w, h, m):
        j = 2 * m + core
        lhs = xin[w, :, half_rows(h), :].reshape(rows * HALF, 2 * width)
        rhs = xin[lax.div(j, rows), lax.rem(j, rows)]
        val = lax.dot_general(lhs, rhs, (((1,), (1,)), ((), ())), preferred_element_type=F32)
        return val.reshape(rows, HALF, BLOCK)

    def x_mid(t, e, d):
        sl = rem(t, slots)
        return remote(part.at[sl, 1, e, (A, B)[d]], xmid.at[sl, d, e],
                      xm_s.at[d, sl, e], xm_r.at[d, sl, e], xdev[d])

    def x_own(t, e, d):
        sl, half = rem(t, slots), (B, A)[d]
        return remote(part.at[sl, 2 * d, e, half], xdst.at[sl, d, e, half],
                      xo_s.at[d, sl, e], xo_r.at[d, sl, e], xdev[d])

    def x_acc(t, e, d):
        sl, half = rem(t, slots), (A, B)[d]
        return remote(part.at[sl, 2 * d, e, half], xdst.at[sl, d, e, half],
                      xa_s.at[d, sl, e], xa_r.at[d, sl, e], xdev[d])

    def x_send_mid(t):
        for e in range(ents):
            when(low(t, 2, e), lambda: x_mid(t, e, 0).start())
            when(high(t, 2, e), lambda: x_mid(t, e, 1).start())

    def x_send_own(t, d):
        for e in range(ents):
            when(high(t, 1, e) if d == 0 else low(t, chips - 1, e), lambda: x_own(t, e, d).start())

    def x_pass_on(t):
        sl = rem(t, slots)
        for e in range(ents):
            for d, o, half, test in ((0, 1, A, low), (1, chips - 1, B, high)):
                def one():
                    arrived(xmid.at[sl, d, e], xm_s.at[d, sl, e], xm_r.at[d, sl, e])
                    part[sl, 2 * d, e, half] += xmid[sl, d, e]
                    x_acc(t, e, d).start()
                when(test(t, o, e), one)

    def x_finish(t):
        sl = rem(t, slots)
        for e in range(ents):
            ix = spot(t, e)

            def first():
                arrived(xdst.at[sl, 0, e, A], xa_s.at[0, sl, e], xa_r.at[0, sl, e])
                arrived(xdst.at[sl, 1, e, A], xo_s.at[1, sl, e], xo_r.at[1, sl, e])
                red[ix, A] = red[ix, A] + xdst[sl, 0, e, A] + xdst[sl, 1, e, A]

            def second():
                arrived(xdst.at[sl, 0, e, B], xo_s.at[0, sl, e], xo_r.at[0, sl, e])
                arrived(xdst.at[sl, 1, e, B], xa_s.at[1, sl, e], xa_r.at[1, sl, e])
                red[ix, B] = red[ix, B] + xdst[sl, 0, e, B] + xdst[sl, 1, e, B]
            when(low(t, 0, e), first)
            when(high(t, 0, e), second)
        if not isinstance(t, int) or t + slots < items:
            signal(credit.at[0], left)
            signal(credit.at[1], right)
        if isinstance(t, int) and t + slots == items - 1:
            signal(credit.at[2], up)
            signal(credit.at[3], down)

    def x_sent(t):
        sl = rem(t, slots)
        for e in range(ents):
            for o, d, half, s, r, test in (
                    (2, 0, A, xm_s, xm_r, low), (2, 1, B, xm_s, xm_r, high),
                    (1, 0, B, xo_s, xo_r, high), (chips - 1, 1, A, xo_s, xo_r, low),
                    (1, 0, A, xa_s, xa_r, low), (chips - 1, 1, B, xa_s, xa_r, high)):
                when(test(t, o, e), lambda: left_us(part.at[sl, o - 1, e, half], s.at[d, sl, e], r.at[d, sl, e]))

    def take_credit(first):
        pl.semaphore_wait(credit.at[first], 1)
        pl.semaphore_wait(credit.at[first + 1], 1)

    def compute(t):
        w, kind, _ = split(t)
        sl = rem(t, slots)

        def twin_in():
            h = 2 * w + kind
            arrived(twin_rows(h, width), core_s.at[h], core_r.at[h])
        when(kind < 2, twin_in)
        when(t >= slots, lambda: x_sent(t - slots))

        def one(i, _):
            n, e = lax.div(i, 2), lax.rem(i, 2)
            o = lax.rem(2 + 3 * n + 3 * lax.div(n, 2) + 2 * lax.div(n, 3), chips)
            m = column(t, o, e)

            @pl.when(high(t, o, e))
            def _():
                h, cb = place(t, e)
                val = product(w, h, m)

                @pl.when(o == 0)
                def _():
                    red[h + late * cb] = val

                @pl.when(o > 0)
                def _():
                    part[sl, o - 1, e] = val

            @pl.when(i == 1)
            def _():
                when(t >= slots, lambda: take_credit(0))
                x_send_mid(t)

            @pl.when(i == 3)
            def _():
                x_send_own(t, 0)

            @pl.when(i == 5)
            def _():
                x_send_own(t, 1)
            return 0

        lax.fori_loop(0, 2 * chips, one, 0)

    T, U = pl.ds(0, QUART), pl.ds(QUART, QUART)
    ahead = (1, rows - 1)

    def exists(t, o, e):
        w, _, own_cols = split(t)
        m = column(t, 0, e)
        return choose(own_cols, m < 2 * w, (lax.div(m, 2) == w) & (rows * w + yy(o) >= 2 * m + core))

    def y_mid(ix, d):
        return remote(red.at[ix, yy(2), (T, U)[d]], ymid.at[ix, d], ym_s.at[d, ix], ym_r.at[d, ix], ydev[d])

    def y_own(ix, d):
        half = (U, T)[d]
        return remote(red.at[ix, yy(ahead[d]), half], ydst.at[ix, d, half], yo_s.at[d, ix], yo_r.at[d, ix], ydev[d])

    def y_acc(ix, d):
        half = (T, U)[d]
        return remote(red.at[ix, yy(ahead[d]), half], ydst.at[ix, d, half], ya_s.at[d, ix], ya_r.at[d, ix], ydev[d])

    def y_send(t):
        for e in range(ents):
            when(exists(t, 2, e), lambda: [y_mid(spot(t, e), d).start() for d in range(2)] and None)
        for e in range(ents):
            for d in range(2):
                when(exists(t, ahead[d], e), lambda: y_own(spot(t, e), d).start())

    def y_pass_on(t):
        for e in range(ents):
            ix = spot(t, e)
            for d in range(2):
                o, half = ahead[d], (T, U)[d]

                def one():
                    arrived(ymid.at[ix, d], ym_s.at[d, ix], ym_r.at[d, ix])
                    red[ix, yy(o), half] += ymid[ix, d]
                    y_acc(ix, d).start()
                when(exists(t, o, e), one)

    def rounded(h, m, val):
        i = (rows * div(h, 2) + y) * BLOCK + rem(h, 2) * HALF + lax.broadcasted_iota(jnp.int32, val.shape, 0)
        j = (2 * m + core) * BLOCK + lax.broadcasted_iota(jnp.int32, val.shape, 1)
        return jnp.where(i >= j, val, 0.0).astype(c_ref.dtype)

    def result(h, cb):
        return (pl.ds(pl.multiple_of(h * HALF, HALF), HALF), pl.ds(pl.multiple_of(cb * BLOCK, BLOCK), BLOCK))

    def to_owner(s):
        return remote(fin.at[0, s], fin.at[1, s], fin_s.at[s], fin_r.at[s], across)

    def y_finish(t):
        for e in range(ents):
            h, cb = place(t, e)
            ix = spot(t, e)

            def one():
                for d in range(2):
                    half, other = (U, T)[d], (T, U)[d]
                    arrived(ydst.at[ix, d, half], yo_s.at[d, ix], yo_r.at[d, ix])
                    arrived(ydst.at[ix, d, other], ya_s.at[d, ix], ya_r.at[d, ix])
                val = rounded(h, column(t, 0, e), red[ix, y] + ydst[ix, 0] + ydst[ix, 1])
                if moved(t) and e == 1:
                    fin[0, t % 3] = val
                    to_owner(t % 3).start()
                else:
                    c_ref[result(h, cb)] = val
            when(exists(t, 0, e), one)

    def from_opposite():
        for s in range(2):
            def one():
                arrived(fin.at[1, s], fin_s.at[s], fin_r.at[s])
                c_ref[result(2 * last + s, 1)] = fin[1, s]
            when(chips + x < 2 * last, one)

    def y_sent(t):
        for e in range(ents):
            ix = spot(t, e)
            for d in range(2):
                o, half, other = ahead[d], (U, T)[d], (T, U)[d]

                def sides():
                    left_us(red.at[ix, yy(o), half], yo_s.at[d, ix], yo_r.at[d, ix])
                    left_us(red.at[ix, yy(o), other], ya_s.at[d, ix], ya_r.at[d, ix])
                when(exists(t, 2, e), lambda: left_us(red.at[ix, yy(2), other], ym_s.at[d, ix], ym_r.at[d, ix]))
                when(exists(t, o, e), sides)

    zs = (items - 1) % slots
    pairs = [(g, e) for g in range(2) for e in range(2)]

    def z_exists(g, o):
        return yy(o) >= 2 * g + core

    def z_mid(g, e, d):
        return remote(part.at[zs, g, e, yy(2), (T, U)[d]], xmid.at[zs, d, e, g, T],
                      zm_s.at[d, g, e], zm_r.at[d, g, e], ydev[d])

    def z_side(g, e, d, half, s, r):
        return remote(part.at[zs, g, e, yy(ahead[d]), half], xdst.at[zs, d, e, g, half],
                      s.at[d, g, e], r.at[d, g, e], ydev[d])

    def z_own(g, e, d):
        return z_side(g, e, d, (U, T)[d], zo_s, zo_r)

    def z_acc(g, e, d):
        return z_side(g, e, d, (T, U)[d], za_s, za_r)

    def away(g):
        return lax.rem((2 * last + g) % chips + chips - x, chips)

    def w_mid(g, e, d):
        return remote(part.at[zs, g, e, y, (T, U)[d]], xmid.at[zs, d, e, 0, U], wm_s.at[d, e], wm_r.at[d, e], xdev[d])

    def w_side(g, e, d, half, s, r):
        return remote(part.at[zs, g, e, y, half], xdst.at[zs, d, e, 2, half], s.at[d, e], r.at[d, e], xdev[d])

    def w_own(g, e, d):
        return w_side(g, e, d, (U, T)[d], wo_s, wo_r)

    def w_acc(g, e, d):
        return w_side(g, e, d, (T, U)[d], wa_s, wa_r)

    def z_compute():
        x_sent(items - 1 - slots)

        def one(i, _):
            g, e = lax.div(i, 2), lax.rem(i, 2)
            part[zs, g, e] = product(last, e, 2 * last + g)
            return 0
        lax.fori_loop(0, 4, one, 0)
        take_credit(2)
        for g, e in pairs:
            when(z_exists(g, 2), lambda: [z_mid(g, e, d).start() for d in range(2)] and None)
        for g, e in pairs:
            for d in range(2):
                when(z_exists(g, ahead[d]), lambda: z_own(g, e, d).start())

    def z_pass_on():
        for g, e in pairs:
            for d in range(2):
                half = (T, U)[d]

                def one():
                    arrived(xmid.at[zs, d, e, g, T], zm_s.at[d, g, e], zm_r.at[d, g, e])
                    part[zs, g, e, yy(ahead[d]), half] += xmid[zs, d, e, g, T]
                    z_acc(g, e, d).start()
                when(z_exists(g, ahead[d]), one)

    def z_turn():
        take_credit(0)
        for g, e in pairs:
            def one():
                for d in range(2):
                    half, other = (U, T)[d], (T, U)[d]
                    arrived(xdst.at[zs, d, e, g, half], zo_s.at[d, g, e], zo_r.at[d, g, e])
                    arrived(xdst.at[zs, d, e, g, other], za_s.at[d, g, e], za_r.at[d, g, e])
                part[zs, g, e, y] = part[zs, g, e, y] + xdst[zs, 0, e, g] + xdst[zs, 1, e, g]
                pl.when(away(g) == 2)(lambda: [w_mid(g, e, d).start() for d in range(2)] and None)
                pl.when(away(g) == 1)(lambda: w_own(g, e, 0).start())
                pl.when(away(g) == chips - 1)(lambda: w_own(g, e, 1).start())
            when(z_exists(g, 0), one)

    def w_pass_on():
        for g, e in pairs:
            for d in range(2):
                half = (T, U)[d]

                def one():
                    arrived(xmid.at[zs, d, e, 0, U], wm_s.at[d, e], wm_r.at[d, e])
                    part[zs, g, e, y, half] += xmid[zs, d, e, 0, U]
                    w_acc(g, e, d).start()
                when(z_exists(g, 0) & (away(g) == (1, chips - 1)[d]), one)

    def w_finish():
        for g, e in pairs:
            def one():
                for d in range(2):
                    half, other = (U, T)[d], (T, U)[d]
                    arrived(xdst.at[zs, d, e, 2, half], wo_s.at[d, e], wo_r.at[d, e])
                    arrived(xdst.at[zs, d, e, 2, other], wa_s.at[d, e], wa_r.at[d, e])
                val = part[zs, g, e, y] + xdst[zs, 0, e, 2] + xdst[zs, 1, e, 2]
                m = 2 * last + g
                c_ref[result(2 * last + e, m // chips)] = rounded(2 * last + e, m, val)
            when(z_exists(g, 0) & (away(g) == 0), one)

    def z_sent():
        for g, e in pairs:
            for d in range(2):
                half, other = (U, T)[d], (T, U)[d]

                def sides():
                    left_us(part.at[zs, g, e, yy(ahead[d]), half], zo_s.at[d, g, e], zo_r.at[d, g, e])
                    left_us(part.at[zs, g, e, yy(ahead[d]), other], za_s.at[d, g, e], za_r.at[d, g, e])

                def w_sides():
                    left_us(part.at[zs, g, e, y, half], wo_s.at[d, e], wo_r.at[d, e])
                    left_us(part.at[zs, g, e, y, other], wa_s.at[d, e], wa_r.at[d, e])
                when(z_exists(g, 2), lambda: left_us(part.at[zs, g, e, yy(2), other], zm_s.at[d, g, e], zm_r.at[d, g, e]))
                when(z_exists(g, ahead[d]), sides)
                when(z_exists(g, 0) & (away(g) == 2),
                     lambda: left_us(part.at[zs, g, e, y, other], wm_s.at[d, e], wm_r.at[d, e]))
                when(z_exists(g, 0) & (away(g) == (1, chips - 1)[d]), w_sides)

    def half_of(t):
        return 2 * div(t, 3) + rem(t, 3)

    def have(t):
        h = half_of(t)
        own(h).wait()
        for d in range(2):
            arrived(x_piece(h, yy(rows - 1 if d == 0 else 1), 0, width), d_s.at[d, h], d_r.at[d, h])
            arrived(x_piece(h, yy(2), d * half_w, half_w), f_s.at[d, h], f_r.at[d, h])
        to_twin(h).start()

    def more(t):
        h = half_of(t)
        when(h + 3 < steps, lambda: both(relay_out, h + 3))

        def forth():
            pass_on(h + 2)
            both(direct, h + 2)
        when(h + 2 < steps, forth)

    def loop(lo, hi, f):
        def body(i, _):
            f(i)
            return 0
        lax.fori_loop(lo, hi, body, 0)

    both(relay_out, 0)
    both(relay_out, 1)
    pass_on(0)
    both(direct, 0)
    both(relay_out, 2)
    loop(0, steps, lambda h: own(h).start())
    c_ref[...] = jnp.zeros_like(c_ref)
    pass_on(1)
    both(direct, 1)

    def step(t):
        when(rem(t, 3) < 2, lambda: have(t))
        compute(t)
        when(rem(t, 3) < 2, lambda: more(t))
        when(t >= 1, lambda: x_pass_on(t - 1))
        when(t >= 2, lambda: x_finish(t - 2))

    loop(0, START, step)

    acts = {"H": have, "G": more, "C": compute, "p": x_pass_on, "f": x_finish, "S": y_send, "P": y_pass_on,
            "F": y_finish, "Z": lambda n: (z_compute, z_pass_on, z_turn, w_pass_on, w_finish)[n]()}
    for act in TAIL:
        acts[act[0]](int(act[1:]))
    from_opposite()

    def drain(h):
        for d in range(2):
            left_us(a_piece(h, yy(1), 0, width), d_s.at[d, h], d_r.at[d, h])
            left_us(a_piece(h, yy(2), 0, half_w), r_s.at[d, h], r_r.at[d, h])
            left_us(relay.at[d, h], f_s.at[d, h], f_r.at[d, h])
        left_us(twin_rows(h, 0), core_s.at[h], core_r.at[h])

    loop(0, steps, drain)
    z_sent()
    for t in range(items - slots, items - 1):
        x_sent(t)
    for s in range(2):
        when(chips + xx(2) < 2 * last, lambda: left_us(fin.at[0, s], fin_s.at[s], fin_r.at[s]))
    loop(0, items - 3, y_sent)
    for t in range(items - 3, items - 1):
        y_sent(t)


def solution(mesh):
    rows, cols = mesh.shape["row"], mesh.shape["col"]

    def local_fn(a_local):
        local_rows, m_local = a_local.shape
        steps, waves = local_rows // HALF, local_rows // BLOCK
        width = m_local // rows
        chips = cols // 2
        cbs = local_rows * rows // (BLOCK * cols)
        slots, spots = 3, steps + steps // 2
        dma = pltpu.SemaphoreType.DMA
        c, _ = pl.pallas_call(
            functools.partial(kernel, rows, cols),
            out_shape=(
                jax.ShapeDtypeStruct((local_rows, cbs * BLOCK), a_local.dtype),
                jax.ShapeDtypeStruct((2, steps, HALF, width // 2), a_local.dtype),
            ),
            in_specs=[pl.BlockSpec(memory_space=pltpu.HBM)],
            out_specs=(pl.BlockSpec(memory_space=pltpu.VMEM), pl.BlockSpec(memory_space=pltpu.HBM)),
            scratch_shapes=[
                pltpu.VMEM((waves, rows, BLOCK, 2 * width), a_local.dtype),
                pltpu.VMEM((slots, chips - 1, cbs, rows, HALF, BLOCK), F32),
                pltpu.VMEM((slots, 2, cbs, 2, HALF, BLOCK), F32),
                pltpu.VMEM((slots, 2, cbs, rows, HALF, BLOCK), F32),
                pltpu.VMEM((spots, rows, HALF, BLOCK), F32),
                pltpu.VMEM((spots, 2, QUART, BLOCK), F32),
                pltpu.VMEM((spots, 2, HALF, BLOCK), F32),
                pltpu.VMEM((2, 2, HALF, BLOCK), a_local.dtype),
            ] + [dma((2, steps))] * 6 + [dma((steps,))] * 3 + [dma((2, slots, cbs))] * 6 + [dma((2, spots))] * 6
            + [dma((2, 2, 2))] * 6 + [dma((2, 2))] * 6 + [dma((2,))] * 2 + [pltpu.SemaphoreType.REGULAR((4,))],
            compiler_params=pltpu.CompilerParams(
                collective_id=0, has_side_effects=True, vmem_limit_bytes=67043328),
        )(a_local)
        return c

    spec = P(("batch", "row"), "col")
    return jax.shard_map(local_fn, mesh=mesh, in_specs=(spec,), out_specs=spec, check_vma=False)
```

time: 2250 us -> 272 us (0.12)
  waiting for transfers between devices: 1810 us -> 0 us
  local copies, waits for them, and re-layouts: 291 us -> 2.26 us
  Pallas kernels: 0 us -> 268 us
  matrix products: 114 us -> 0 us
    all_to_all x1 -> x0, waiting for transfers between devices: 1240 us -> none  [local_fn(): swapped = lax.all_to_all(grouped, 'col', 1, 3, tiled=True)]
    all_gather x2 -> x0, waiting for transfers between devices: 574 us -> none  [the longest x1 574 us: local_fn(): lax.all_gather(a_local.reshape(local_rows // BLOCK, BLOCK, m_local), 'row...]
    pallas_call x0 -> x1, Pallas kernels: none -> 268 us  [local_fn(): pl.pallas_call(functools.partial(kernel, rows, cols), out_shape=(jax.Shap...]
    all_to_all x2 -> x0, local copies, waits for them, and re-layouts: 168 us -> none  [local_fn(): swapped = lax.all_to_all(grouped, 'col', 1, 3, tiled=True)]
    dot_general x4 -> x0, matrix products: 114 us -> none  [lower_part(): lax.dot_general(row_panel[first_blk * BLOCK:last_blk * BLOCK], col_panel[...]
    unnamed x11 -> x1, local copies, waits for them, and re-layouts: 56.1 us -> 2.26 us
    reshape x1 -> x0, local copies, waits for them, and re-layouts: 44.6 us -> none  [local_fn(): gathered.reshape(n_total // (BLOCK * col_count), col_count, BLOCK, m_local)]
    slice x2 -> x0, local copies, waits for them, and re-layouts: 22.8 us -> none  [the longest x1 22.8 us: lower_part(): col_panel[:col_width]]
  transfers between devices with their start and end apart: 3 -> 0, of which waited for: 2 -> 0; matrix products, arithmetic and copies ran while one was open for 13% -> 0% of each run, Pallas kernels for 0% -> 0%
where the time goes in v2:
time: 272 us; the launch traced here: 271 us
  Pallas kernels  268 us (99%)
    pallas_call x1, Pallas kernels, local_fn(): pl.pallas_call(functools.partial(kernel, rows, cols), out_shape=(jax.Shap...  268 us

profile of v2, /device:TPU:98, one launch (start us, length us, event | category | flops | bytes accessed | tf_op | source)
XLA Modules:
  0.0 270.5 jit_solution(1832785169879086009)
XLA Ops:
  0.0 268.2 %shard_map.17 = (bf16[1024,512]{1,0:T(8,128)(2,1)}, bf16[2,8,128,1024]{3,2,1,0:T(8,128)(2,1)}) custom-call(bf16[1024,8192]{1,0:T(8,128)(2,1)} %a_ref.1), custom_call_target="tpu_custom_call" | custom-call | tf_op jit(solution)/shard_map/pallas_call | solution.py:560
  268.3 2.3 copy.3

commit v3 on v2

--- a/solution.py
+++ b/solution.py
@@ -12,11 +12,13 @@
 QUART = BLOCK // 4
 MESH = pl.DeviceIdType.MESH
 F32 = jnp.float32
-START = 8
+START = 6
 TAIL = (
-    "S5", "H9", "p7", "C8", "S2", "G9", "f6", "C9", "S3", "H10", "f7", "S7", "S4", "P3", "p8", "S6", "p9",
-    "C10", "P5", "f8", "Z0", "F5", "P4", "P2", "p10", "f9", "F3", "S8", "Z1", "P6", "F2", "P8", "S9", "f10",
-    "S10", "Z2", "P9", "Z3", "F4", "P10", "P7", "F9", "F8", "F6", "F10", "Z4", "F7",
+    "p5", "H6", "G6", "C6", "H7", "f4", "f5", "p6", "C7", "G7", "f6", "C8", "H9", "S4", "p7", "C9", "f7",
+    "S3", "G9", "p9b", "S6", "H10", "P3", "P6", "p8", "S2", "p9a", "S7", "P2", "C10", "P7", "P4", "f8", "S8",
+    "Z0", "f9a", "p10b", "S5", "P8", "Z1", "f9b", "S9a", "F6", "P5", "S9b", "F2", "p10a", "P9a", "f10b",
+    "F5", "S10b", "P10b", "Z2", "P9b", "f10a", "S10a", "F8", "F10b", "F9b", "Z3", "F7", "F9a", "P10a", "F3",
+    "F10a", "Z4", "F4",
 )
 
 
@@ -36,6 +38,7 @@
     last = steps // 2 - 1
     late = steps - steps // 2
     slots, ents = part.shape[0], part.shape[2]
+    every = tuple(range(ents))
 
     def div(p, q):
         return p // q if isinstance(p, int) else lax.div(p, q)
@@ -177,17 +180,17 @@
                       xa_s.at[d, sl, e], xa_r.at[d, sl, e], xdev[d])
 
     def x_send_mid(t):
-        for e in range(ents):
+        for e in reversed(every) if moved(t) else every:
             when(low(t, 2, e), lambda: x_mid(t, e, 0).start())
             when(high(t, 2, e), lambda: x_mid(t, e, 1).start())
 
     def x_send_own(t, d):
-        for e in range(ents):
+        for e in reversed(every) if moved(t) else every:
             when(high(t, 1, e) if d == 0 else low(t, chips - 1, e), lambda: x_own(t, e, d).start())
 
-    def x_pass_on(t):
+    def x_pass_on(t, es=every):
         sl = rem(t, slots)
-        for e in range(ents):
+        for e in es:
             for d, o, half, test in ((0, 1, A, low), (1, chips - 1, B, high)):
                 def one():
                     arrived(xmid.at[sl, d, e], xm_s.at[d, sl, e], xm_r.at[d, sl, e])
@@ -195,9 +198,9 @@
                     x_acc(t, e, d).start()
                 when(test(t, o, e), one)
 
-    def x_finish(t):
+    def x_finish(t, es=every):
         sl = rem(t, slots)
-        for e in range(ents):
+        for e in es:
             ix = spot(t, e)
 
             def first():
@@ -242,7 +245,7 @@
         when(t >= slots, lambda: x_sent(t - slots))
 
         def one(i, _):
-            n, e = lax.div(i, 2), lax.rem(i, 2)
+            n, e = lax.div(i, 2), 1 - lax.rem(i, 2) if moved(t) else lax.rem(i, 2)
             o = lax.rem(2 + 3 * n + 3 * lax.div(n, 2) + 2 * lax.div(n, 3), chips)
             m = column(t, o, e)
 
@@ -294,15 +297,15 @@
         half = (T, U)[d]
         return remote(red.at[ix, yy(ahead[d]), half], ydst.at[ix, d, half], ya_s.at[d, ix], ya_r.at[d, ix], ydev[d])
 
-    def y_send(t):
-        for e in range(ents):
+    def y_send(t, es=every):
+        for e in es:
             when(exists(t, 2, e), lambda: [y_mid(spot(t, e), d).start() for d in range(2)] and None)
-        for e in range(ents):
+        for e in es:
             for d in range(2):
                 when(exists(t, ahead[d], e), lambda: y_own(spot(t, e), d).start())
 
-    def y_pass_on(t):
-        for e in range(ents):
+    def y_pass_on(t, es=every):
+        for e in es:
             ix = spot(t, e)
             for d in range(2):
                 o, half = ahead[d], (T, U)[d]
@@ -324,8 +327,8 @@
     def to_owner(s):
         return remote(fin.at[0, s], fin.at[1, s], fin_s.at[s], fin_r.at[s], across)
 
-    def y_finish(t):
-        for e in range(ents):
+    def y_finish(t, es=every):
+        for e in es:
             h, cb = place(t, e)
             ix = spot(t, e)
 
@@ -490,12 +493,12 @@
 
     def more(t):
         h = half_of(t)
-        when(h + 3 < steps, lambda: both(relay_out, h + 3))
-
-        def forth():
-            pass_on(h + 2)
+        when(h + 1 < steps, lambda: pass_on(h + 1))
+
+        def new():
+            both(relay_out, h + 2)
             both(direct, h + 2)
-        when(h + 2 < steps, forth)
+        when(h + 2 < steps, new)
 
     def loop(lo, hi, f):
         def body(i, _):
@@ -504,13 +507,11 @@
         lax.fori_loop(lo, hi, body, 0)
 
     both(relay_out, 0)
-    both(relay_out, 1)
-    pass_on(0)
     both(direct, 0)
-    both(relay_out, 2)
     loop(0, steps, lambda h: own(h).start())
     c_ref[...] = jnp.zeros_like(c_ref)
-    pass_on(1)
+    pass_on(0)
+    both(relay_out, 1)
     both(direct, 1)
 
     def step(t):
@@ -525,7 +526,10 @@
     acts = {"H": have, "G": more, "C": compute, "p": x_pass_on, "f": x_finish, "S": y_send, "P": y_pass_on,
             "F": y_finish, "Z": lambda n: (z_compute, z_pass_on, z_turn, w_pass_on, w_finish)[n]()}
     for act in TAIL:
-        acts[act[0]](int(act[1:]))
+        if act[-1] in "ab":
+            acts[act[0]](int(act[1:-1]), ("ab".index(act[-1]),))
+        else:
+            acts[act[0]](int(act[1:]))
     from_opposite()
 
     def drain(h):

time: 272 us -> 259 us (0.952)
  Pallas kernels: 268 us -> 257 us
    pallas_call x1, Pallas kernels: 268 us -> 257 us  [local_fn(): pl.pallas_call(functools.partial(kernel, rows, cols), out_shape=(jax.Shap...]
where the time goes in v3:
time: 259 us
  Pallas kernels  257 us (99%)
    pallas_call x1, Pallas kernels, local_fn(): pl.pallas_call(functools.partial(kernel, rows, cols), out_shape=(jax.Shap...  257 us

profile of v3, /device:TPU:98, one launch (start us, length us, event | category | flops | bytes accessed | tf_op | source)
XLA Modules:
  0.0 258.9 jit_solution(2156468127418510416)
XLA Ops:
  0.0 256.7 %shard_map.17 = (bf16[1024,512]{1,0:T(8,128)(2,1)}, bf16[2,8,128,1024]{3,2,1,0:T(8,128)(2,1)}) custom-call(bf16[1024,8192]{1,0:T(8,128)(2,1)} %a_ref.1), custom_call_target="tpu_custom_call" | custom-call | tf_op jit(solution)/shard_map/pallas_call | solution.py:564
  256.7 2.3 copy.3

commit v4 on v3

--- a/solution.py
+++ b/solution.py
@@ -14,10 +14,10 @@
 F32 = jnp.float32
 START = 6
 TAIL = (
-    "p5", "H6", "G6", "C6", "H7", "f4", "f5", "p6", "C7", "G7", "f6", "C8", "H9", "S4", "p7", "C9", "f7",
-    "S3", "G9", "p9b", "S6", "H10", "P3", "P6", "p8", "S2", "p9a", "S7", "P2", "C10", "P7", "P4", "f8", "S8",
-    "Z0", "f9a", "p10b", "S5", "P8", "Z1", "f9b", "S9a", "F6", "P5", "S9b", "F2", "p10a", "P9a", "f10b",
-    "F5", "S10b", "P10b", "Z2", "P9b", "f10a", "S10a", "F8", "F10b", "F9b", "Z3", "F7", "F9a", "P10a", "F3",
+    "p5", "H6", "G6", "C6", "f4", "H7", "f5", "p6", "C7", "G7", "f6", "C8", "H9", "S4", "p7", "C9", "f7",
+    "S3", "G9", "p9b", "S6", "H10", "S7", "P6", "P3", "p8", "S2", "p9a", "C10", "P7", "f8", "S8", "P4", "P2",
+    "Z0", "f9a", "Z1", "f9b", "S9a", "p10b", "S5", "P8", "P5", "S9b", "F6", "F2", "p10a", "P9a", "f10b",
+    "S10b", "P10b", "F5", "Z2", "P9b", "f10a", "F8", "S10a", "F10b", "F9b", "Z3", "F7", "F9a", "P10a", "F3",
     "F10a", "Z4", "F4",
 )
 

time: 259 us -> 258 us (level)
  Pallas kernels: 257 us -> 254 us
where the time goes in v4:
time: 258 us; the launch traced here: 257 us
  Pallas kernels  254 us (98%)
    pallas_call x1, Pallas kernels, local_fn(): pl.pallas_call(functools.partial(kernel, rows, cols), out_shape=(jax.Shap...  254 us

profile of v4, /device:TPU:98, one launch (start us, length us, event | category | flops | bytes accessed | tf_op | source)
XLA Modules:
  0.0 256.5 jit_solution(8938942450724879945)
XLA Ops:
  0.0 254.3 %shard_map.17 = (bf16[1024,512]{1,0:T(8,128)(2,1)}, bf16[2,8,128,1024]{3,2,1,0:T(8,128)(2,1)}) custom-call(bf16[1024,8192]{1,0:T(8,128)(2,1)} %a_ref.1), custom_call_target="tpu_custom_call" | custom-call | tf_op jit(solution)/shard_map/pallas_call | solution.py:564
  254.3 2.3 copy.3
